TPU v7x, 32 devices: a whole 2x2x4 slice. The times are simulated.
32 devices in a mesh: gx: 8 (over z, x), gz: 4 (over y, core).
Axes of the slice: x: 2, y: 2, z: 4, core: 2. Of those that a mesh axis runs over, the one named last changes fastest.
Arguments:
- velocity: float32 [3, 64, 128, 384], P(None, 'gx', 'gz'), may hold values from -6 to 6
- y_gap: float32 [385], replicated, may hold values from 0.2 to 2
Outputs:
- eddy_visc: float32 [64, 128, 384], P('gx', 'gz')
- lm_field: float32 [64, 128, 384], P('gx', 'gz')
- mm_field: float32 [64, 128, 384], P('gx', 'gz')
- coefficient: float32 [384], replicated
All inputs are finite; a program needn't handle non-finite values.
Results may differ from a plain program's by a relative error of at most 0.00002.
Values sent between devices are 32-bit elements; how exact they have to be, the bound alone decides.
A program may use at most 64 MiB of HBM per device.

v0:
```python
import jax
import jax.numpy as jnp
from jax import lax
from jax.sharding import PartitionSpec as P

WEIGHTS = (1.0, 1.0, 1.0, 2.0, 2.0, 2.0)


def extended(array, sides, width):
    for axis, dim in sides:
        size, length = (lax.axis_size(axis), array.shape[dim])
        up = [(i, (i + 1) % size) for i in range(size)]
        down = [(j, i) for i, j in up]
        last = lax.slice_in_dim(array, length - width, length, axis=dim)
        leading = lax.slice_in_dim(array, 0, width, axis=dim)
        before = lax.ppermute(last, axis, up)
        after = lax.ppermute(leading, axis, down)
        array = jnp.concatenate([before, array, after], axis=dim)
    return array


def wall_slope(values, y_gap):
    padded = jnp.pad(values, [(0, 0)] * (values.ndim - 1) + [(1, 1)])
    return (padded[..., 2:] - padded[..., :-2]) / (y_gap[:-1] + y_gap[1:])


def strain_parts(slope_x, slope_y, slope_z):
    return jnp.stack(
        [
            slope_x[0],
            slope_y[1],
            slope_z[2],
            0.5 * (slope_y[0] + slope_x[1]),
            0.5 * (slope_z[0] + slope_x[2]),
            0.5 * (slope_z[1] + slope_y[2]),
        ]
    )


def contract(first_part, second_part):
    summed = first_part[0] * second_part[0]
    for component in range(1, 6):
        summed = summed + WEIGHTS[component] * first_part[component] * second_part[component]
    return summed


def magnitude(strain):
    return jnp.sqrt(2.0 * contract(strain, strain))


def pair_products(speeds):
    return jnp.stack(
        [
            speeds[0] * speeds[0],
            speeds[1] * speeds[1],
            speeds[2] * speeds[2],
            speeds[0] * speeds[1],
            speeds[0] * speeds[2],
            speeds[1] * speeds[2],
        ]
    )


def width_square(y_gap):
    return (0.5 * (y_gap[:-1] + y_gap[1:])) ** (2.0 / 3.0)


def germano(smooth_velocity, smooth_pairs, smooth_stress, test_strain, width_sq):
    leonard = smooth_pairs - pair_products(smooth_velocity)
    model_term = 2.0 * width_sq * (smooth_stress - 4.0 * magnitude(test_strain) * test_strain)
    return (contract(leonard, model_term), contract(model_term, model_term))


def rim_strain(padded, y_gap):
    slope_x = (padded[:, 2:, 1:-1] - padded[:, :-2, 1:-1]) * 0.5
    slope_z = (padded[:, 1:-1, 2:] - padded[:, 1:-1, :-2]) * 0.5
    slope_y = wall_slope(padded[:, 1:-1, 1:-1], y_gap)
    return strain_parts(slope_x, slope_y, slope_z)


def rim_filter(values):
    along_x = 0.25 * values[:, :-2] + 0.5 * values[:, 1:-1] + 0.25 * values[:, 2:]
    return 0.25 * along_x[:, :, :-2] + 0.5 * along_x[:, :, 1:-1] + 0.25 * along_x[:, :, 2:]


def per_device(velocity, y_gap):
    width_sq = width_square(y_gap)
    padded = extended(velocity, (("gx", 1), ("gz", 2)), 2)
    strain_wide = rim_strain(padded, y_gap)
    size_wide = magnitude(strain_wide)
    inner = padded[:, 1:-1, 1:-1]
    smooth_pairs = rim_filter(pair_products(inner))
    smooth_stress = rim_filter(size_wide * strain_wide)
    smooth_wide = rim_filter(padded)
    smooth_velocity = smooth_wide[:, 1:-1, 1:-1]
    test_strain = rim_strain(smooth_wide, y_gap)
    strain_size = size_wide[1:-1, 1:-1]
    lm_field, mm_field = germano(
        smooth_velocity, smooth_pairs, smooth_stress, test_strain, width_sq
    )
    planes = velocity.shape[1] * lax.axis_size("gx") * velocity.shape[2] * lax.axis_size("gz")
    plane_pair = jnp.stack([jnp.sum(lm_field, axis=(0, 1)), jnp.sum(mm_field, axis=(0, 1))])
    total_pair = lax.psum(plane_pair, ("gx", "gz"))
    coefficient = total_pair[0] / planes / (total_pair[1] / planes + 1e-06)
    eddy_visc = coefficient * width_sq * strain_size
    return (eddy_visc, lm_field, mm_field, coefficient)


def solution(mesh):
    placed = (P(None, "gx", "gz", None), P())
    return jax.shard_map(
        per_device,
        mesh=mesh,
        in_specs=placed,
        out_specs=(P("gx", "gz", None), P("gx", "gz", None), P("gx", "gz", None), P()),
        check_vma=False,
    )
```

profile of v0, /device:TPU:0, one launch (start us, length us, event | category | flops | bytes accessed | tf_op | source)
XLA Modules:
  0.0 76.4 jit_solution(4850961541052591493)
XLA Ops:
  0.7 1.2 %fusion.70 = (f32[3,2,32,384]{3,2,1,0:T(8,128)S(1)}, f32[3,2,32,384]{3,2,1,0:T(8,128)S(1)}) fusion(f32[3,8,32,384]{3,2,1,0:T(8,128)} %param.2), kind=kLoop, calls=%fused_computation.159 | loop fusion | bytes 1179648 | tf_op jit(solution)/shard_map/slice | solution.py:15
  1.8 3.0 %collective-permute-start = (f32[3,2,32,384]{3,2,1,0:T(8,128)S(1)}, f32[3,2,32,384]{3,2,1,0:T(8,128)S(1)}, u32[]{:S(2)}, u32[]{:S(2)}) collective-permute-start(f32[3,2,32,384]{3,2,1,0:T(8,128)S(1)} %get-tuple-element.30), channel_id=1, source_target_pairs={{0,4},{4,8},{8,12},{12,16},{16,20},{20,24},{24,28},{28,0},{1,5},{5... | collective-permute-start | bytes 884744 | tf_op jit(solution)/shard_map/ppermute | solution.py:16
  4.9 3.1 %collective-permute-start.1 = (f32[3,2,32,384]{3,2,1,0:T(8,128)S(1)}, f32[3,2,32,384]{3,2,1,0:T(8,128)S(1)}, u32[]{:S(2)}, u32[]{:S(2)}) collective-permute-start(f32[3,2,32,384]{3,2,1,0:T(8,128)S(1)} %get-tuple-element.29), channel_id=1, source_target_pairs={{4,0},{8,4},{12,8},{16,12},{20,16},{24,20},{28,24},{0,28},{5,1},{9... | collective-permute-start | bytes 884744 | tf_op jit(solution)/shard_map/ppermute | solution.py:17
  8.0 9.5 %collective-permute-done = f32[3,2,32,384]{3,2,1,0:T(8,128)S(1)} collective-permute-done((f32[3,2,32,384]{3,2,1,0:T(8,128)S(1)}, f32[3,2,32,384]{3,2,1,0:T(8,128)S(1)}, u32[]{:S(2)}, u32[]{:S(2)}) %collective-permute-start) | collective-permute-done | bytes 294944 | tf_op jit(solution)/shard_map/ppermute | solution.py:16
  17.5 0.1 constant_dynamic-update-slice_fusion.1
  17.6 2.1 %collective-permute-done.1 = f32[3,2,32,384]{3,2,1,0:T(8,128)S(1)} collective-permute-done((f32[3,2,32,384]{3,2,1,0:T(8,128)S(1)}, f32[3,2,32,384]{3,2,1,0:T(8,128)S(1)}, u32[]{:S(2)}, u32[]{:S(2)}) %collective-permute-start.1) | collective-permute-done | bytes 294944 | tf_op jit(solution)/shard_map/ppermute | solution.py:17
  19.8 0.5 collective-permute-start.2
  20.3 0.1 fusion.58
  20.4 1.8 %collective-permute-done.3 = f32[3,12,2,384]{3,2,1,0:T(2,128)S(1)} collective-permute-done((f32[3,12,2,384]{3,2,1,0:T(2,128)S(1)}, f32[3,12,2,384]{3,2,1,0:T(2,128)S(1)}, u32[]{:S(2)}, u32[]{:S(2)}) %collective-permute-start.3) | collective-permute-done | bytes 110624 | tf_op jit(solution)/shard_map/ppermute | solution.py:17
  22.3 3.0 %collective-permute-done.2 = f32[3,12,2,384]{3,2,1,0:T(2,128)S(1)} collective-permute-done((f32[3,12,2,384]{3,2,1,0:T(2,128)S(1)}, f32[3,12,2,384]{3,2,1,0:T(2,128)S(1)}, u32[]{:S(2)}, u32[]{:S(2)}) %collective-permute-start.2) | collective-permute-done | bytes 110624 | tf_op jit(solution)/shard_map/ppermute | solution.py:16
  25.2 0.3 pad_maximum_fusion
  25.5 0.3 fusion.15
  25.8 0.3 fusion.18
  26.0 0.5 fusion.16
  26.6 0.4 fusion.22
  27.1 1.3 %fusion.12 = (f32[3,10,34,384]{3,2,1,0:T(8,128)S(1)}, f32[3,10,34,384]{3,2,1,0:T(8,128)S(1)}) fusion(f32[3,10,34,384]{3,2,1,0:T(8,128)S(1)} %get-tuple-element.22, f32[384]{0:T(512)S(1)} %get-tuple-element.9, f32[3,12,32,384]{3,2,1,0:T(8,128)S(1)} %constant_dynamic-update-slice_fusion, f32[3,12,2,384]{3,2,1,0:T(2,128)S(1)} %collective-permute-done.2, ...), kind=kLoop, calls=%fused_computation.27 | loop fusion | flops 2350080 | bytes 6692352 | tf_op jit(solution)/shard_map/div | solution.py:24
  28.5 0.6 fusion.29
  29.2 0.1 multiply_dynamic-update-slice_fusion.1
  29.3 0.1 multiply_dynamic-update-slice_fusion
  29.4 0.3 broadcast_multiply_fusion
  29.6 0.4 fusion
  30.1 0.7 fusion.21
  30.8 0.4 fusion.36
  31.8 0.1 multiply_dynamic-update-slice_fusion.5
  31.9 0.1 multiply_dynamic-update-slice_fusion.4
  32.0 0.1 multiply_dynamic-update-slice_fusion.3
  32.2 0.4 fusion.2
  32.6 0.9 %fusion.9 = f32[6,8,32,384]{3,2,1,0:T(8,128)S(1)} fusion(f32[6,8,32,384]{3,2,1,0:T(8,128)S(1)} %multiply_dynamic-update-slice_fusion.12, f32[6,8,34,384]{3,2,1,0:T(8,128)S(1)} %fusion.2), kind=kLoop, calls=%fused_computation.21 | loop fusion | flops 3538944 | bytes 11796480 | tf_op jit(solution)/shard_map/sub | solution.py:69
  33.5 0.9 %fusion.6 = f32[6,8,32,384]{3,2,1,0:T(8,128)S(1)} fusion(f32[6,8,34,384]{3,2,1,0:T(8,128)S(1)} %fusion, f32[6,8,32,384]{3,2,1,0:T(8,128)S(1)} %multiply_dynamic-update-slice_fusion.9, f32[8,32,384]{2,1,0:T(8,128)S(1)} %get-tuple-element.19, f32[384]{0:T(512)S(1)} %get-tuple-element.8), kind=kLoop, calls=%fused_computation.15 | loop fusion | flops 4718592 | bytes 12191232 | tf_op jit(solution)/shard_map/mul | solution.py:70
  34.4 1.4 %fusion.65 = (f32[384]{0:T(512)S(1)}, f32[8,32,384]{2,1,0:T(8,128)}, f32[384]{0:T(512)S(1)}, f32[8,32,384]{2,1,0:T(8,128)}) fusion(f32[6,8,32,384]{3,2,1,0:T(8,128)S(1)} %fusion.6, f32[6,8,32,384]{3,2,1,0:T(8,128)S(1)} %fusion.9), kind=kLoop, calls=%fused_computation.156 | loop fusion | flops 2948352 | bytes 5508096 | tf_op jit(solution)/shard_map/reduce_sum | solution.py:102
  35.8 39.4 %psum.7 = f32[2,384]{1,0:T(2,128)S(1)} all-reduce(f32[2,384]{1,0:T(2,128)S(1)} %pad_maximum_fusion.3), channel_id=1, replica_groups=mesh['gx'=8,'gz'=4] {'gx','gz'}, use_global_device_ids=true, to_apply=%region_2.3 | all-reduce | flops 768 | bytes 6144 | tf_op jit(solution)/shard_map/psum | solution.py:103
  75.2 1.1 %fusion.44 = f32[8,32,384]{2,1,0:T(8,128)} fusion(f32[10,34,384]{2,1,0:T(8,128)S(1)} %get-tuple-element.14, f32[10,34,384]{2,1,0:T(8,128)S(1)} %get-tuple-element.12, f32[10,34,384]{2,1,0:T(8,128)S(1)} %get-tuple-element.16, f32[10,34,384]{2,1,0:T(8,128)S(1)} %broadcast_multiply_fusion.1, f32[10,34,384]{2,1,0:T(8,128)S(1)} %bitcast.69, f32[384]{0:T(512)S(1)} %fusion.57), kind=kLoop, calls=%fused_computation.103 | loop fusion | flops 983040 | bytes 2360832 | tf_op jit(solution)/shard_map/mul | solution.py:105
  (33 shorter events, 1.1 us)
Async XLA Ops:
  0.6 16.8 %copy-start = (f32[3,8,32,384]{3,2,1,0:T(8,128)S(1)}, f32[3,8,32,384]{3,2,1,0:T(8,128)}, u32[]{:S(2)}) copy-start(f32[3,8,32,384]{3,2,1,0:T(8,128)} %param.2) | copy-start | bytes 3538948
  0.6 19.7 %copy-start.2 = (f32[385]{0:T(512)S(1)}, f32[385]{0:T(512)}, u32[]{:S(2)}) copy-start(f32[385]{0:T(512)} %param.3) | copy-start | bytes 4624
  1.8 15.6 %collective-permute-start = (f32[3,2,32,384]{3,2,1,0:T(8,128)S(1)}, f32[3,2,32,384]{3,2,1,0:T(8,128)S(1)}, u32[]{:S(2)}, u32[]{:S(2)}) collective-permute-start(f32[3,2,32,384]{3,2,1,0:T(8,128)S(1)} %get-tuple-element.30), channel_id=1, source_target_pairs={{0,4},{4,8},{8,12},{12,16},{16,20},{20,24},{24,28},{28,0},{1,5},{5... | collective-permute-start | bytes 884744 | tf_op jit(solution)/shard_map/ppermute | solution.py:16
  4.9 14.8 %collective-permute-start.1 = (f32[3,2,32,384]{3,2,1,0:T(8,128)S(1)}, f32[3,2,32,384]{3,2,1,0:T(8,128)S(1)}, u32[]{:S(2)}, u32[]{:S(2)}) collective-permute-start(f32[3,2,32,384]{3,2,1,0:T(8,128)S(1)} %get-tuple-element.29), channel_id=1, source_target_pairs={{4,0},{8,4},{12,8},{16,12},{20,16},{24,20},{28,24},{0,28},{5,1},{9... | collective-permute-start | bytes 884744 | tf_op jit(solution)/shard_map/ppermute | solution.py:17
  19.8 2.5 %collective-permute-start.3 = (f32[3,12,2,384]{3,2,1,0:T(2,128)S(1)}, f32[3,12,2,384]{3,2,1,0:T(2,128)S(1)}, u32[]{:S(2)}, u32[]{:S(2)}) collective-permute-start(f32[3,12,2,384]{3,2,1,0:T(2,128)S(1)} %get-tuple-element.28), channel_id=1, source_target_pairs={{1,0},{2,1},{3,2},{0,3},{5,4},{6,5},{7,6},{4,7},{9,8},{10,9},{11,1... | collective-permute-start | bytes 331784 | tf_op jit(solution)/shard_map/ppermute | solution.py:17
  19.8 5.4 %collective-permute-start.2 = (f32[3,12,2,384]{3,2,1,0:T(2,128)S(1)}, f32[3,12,2,384]{3,2,1,0:T(2,128)S(1)}, u32[]{:S(2)}, u32[]{:S(2)}) collective-permute-start(f32[3,12,2,384]{3,2,1,0:T(2,128)S(1)} %get-tuple-element.27), channel_id=1, source_target_pairs={{0,1},{1,2},{2,3},{3,0},{4,5},{5,6},{6,7},{7,4},{8,9},{9,10},{10,1... | collective-permute-start | bytes 331784 | tf_op jit(solution)/shard_map/ppermute | solution.py:16
  75.2 1.2 %copy-start.1 = (f32[384]{0:T(512)}, f32[384]{0:T(512)S(1)}, u32[]{:S(2)}) copy-start(f32[384]{0:T(512)S(1)} %fusion.61) | copy-start | bytes 4612
where the time goes:
time: 76.6 us; the launch traced here: 76.4 us
  blocking collectives  39.4 us (51%)
  waiting for transfers between devices  16.4 us (21%)
  other arithmetic  11.4 us (15%)
  starting transfers between devices  6.68 us (9%)
  local copies, waits for them, and re-layouts  1.59 us (2%)
  between operations  0.97 us (1%)
    psum x1, blocking collectives, per_device(): total_pair = lax.psum(plane_pair, ('gx', 'gz'))  39.4 us
    ppermute x2, waiting for transfers between devices, extended(): before = lax.ppermute(last, axis, up)  12.4 us
    ppermute x2, waiting for transfers between devices, extended(): after = lax.ppermute(leading, axis, down)  3.91 us
    ppermute x2, starting transfers between devices, extended(): before = lax.ppermute(last, axis, up)  3.52 us
    ppermute x2, starting transfers between devices, extended(): after = lax.ppermute(leading, axis, down)  3.16 us
    div x2, other arithmetic, wall_slope(): return (padded[..., 2:] - padded[..., :-2]) / (y_gap[:-1] + y_gap[1:])  1.94 us
  transfers between devices with their start and end apart: 4, of which 4 were waited for; matrix products, arithmetic and copies ran while one was open for 0% of the time, Pallas kernels for 0%

commit v1 on v0

--- a/solution.py
+++ b/solution.py
@@ -1,9 +1,19 @@
+import functools
 import jax
 import jax.numpy as jnp
 from jax import lax
 from jax.sharding import PartitionSpec as P
 
 WEIGHTS = (1.0, 1.0, 1.0, 2.0, 2.0, 2.0)
+
+
+def fill_streams_on(block_in, across):
+    passed = jax.lax.all_gather(block_in, across)
+    lower = jnp.sum(passed, 0)
+    return lower
+
+
+_scan_series = functools.partial(fill_streams_on, across=("gx", "gz"))
 
 
 def extended(array, sides, width):
@@ -100,7 +110,7 @@
     )
     planes = velocity.shape[1] * lax.axis_size("gx") * velocity.shape[2] * lax.axis_size("gz")
     plane_pair = jnp.stack([jnp.sum(lm_field, axis=(0, 1)), jnp.sum(mm_field, axis=(0, 1))])
-    total_pair = lax.psum(plane_pair, ("gx", "gz"))
+    total_pair = _scan_series(plane_pair)
     coefficient = total_pair[0] / planes / (total_pair[1] / planes + 1e-06)
     eddy_visc = coefficient * width_sq * strain_size
     return (eddy_visc, lm_field, mm_field, coefficient)

time: 76.6 us -> 77.3 us (level)
    all_gather x0 -> x1, blocking collectives: none -> 40.1 us  [fill_streams_on(): passed = jax.lax.all_gather(block_in, across)]
    psum x1 -> x0, blocking collectives: 39.4 us -> none  [per_device(): total_pair = lax.psum(plane_pair, ('gx', 'gz'))]
where the time goes in v1:
time: 77.3 us; the launch traced here: 77.1 us
  blocking collectives  40.1 us (52%)
  waiting for transfers between devices  16.4 us (21%)
  other arithmetic  11.5 us (15%)
  starting transfers between devices  6.68 us (9%)
  local copies, waits for them, and re-layouts  1.59 us (2%)
  between operations  0.96 us (1%)
    all_gather x1, blocking collectives, fill_streams_on(): passed = jax.lax.all_gather(block_in, across)  40.1 us
    ppermute x2, waiting for transfers between devices, extended(): before = lax.ppermute(last, axis, up)  12.4 us
    ppermute x2, waiting for transfers between devices, extended(): after = lax.ppermute(leading, axis, down)  3.91 us
    ppermute x2, starting transfers between devices, extended(): before = lax.ppermute(last, axis, up)  3.52 us
    ppermute x2, starting transfers between devices, extended(): after = lax.ppermute(leading, axis, down)  3.16 us
    div x2, other arithmetic, wall_slope(): return (padded[..., 2:] - padded[..., :-2]) / (y_gap[:-1] + y_gap[1:])  1.94 us
  transfers between devices with their start and end apart: 4, of which 4 were waited for; matrix products, arithmetic and copies ran while one was open for 0% of the time, Pallas kernels for 0%

profile of v1, /device:TPU:0, one launch (start us, length us, event | category | flops | bytes accessed | tf_op | source)
XLA Modules:
  0.0 77.1 jit_solution(4728190419374331492)
XLA Ops:
  0.7 1.2 %fusion.70 = (f32[3,2,32,384]{3,2,1,0:T(8,128)S(1)}, f32[3,2,32,384]{3,2,1,0:T(8,128)S(1)}) fusion(f32[3,8,32,384]{3,2,1,0:T(8,128)} %param.2), kind=kLoop, calls=%fused_computation.159 | loop fusion | bytes 1179648 | tf_op jit(solution)/shard_map/slice | solution.py:25
  1.8 3.0 %collective-permute-start = (f32[3,2,32,384]{3,2,1,0:T(8,128)S(1)}, f32[3,2,32,384]{3,2,1,0:T(8,128)S(1)}, u32[]{:S(2)}, u32[]{:S(2)}) collective-permute-start(f32[3,2,32,384]{3,2,1,0:T(8,128)S(1)} %get-tuple-element.30), channel_id=1, source_target_pairs={{0,4},{4,8},{8,12},{12,16},{16,20},{20,24},{24,28},{28,0},{1,5},{5... | collective-permute-start | bytes 884744 | tf_op jit(solution)/shard_map/ppermute | solution.py:26
  4.9 3.1 %collective-permute-start.1 = (f32[3,2,32,384]{3,2,1,0:T(8,128)S(1)}, f32[3,2,32,384]{3,2,1,0:T(8,128)S(1)}, u32[]{:S(2)}, u32[]{:S(2)}) collective-permute-start(f32[3,2,32,384]{3,2,1,0:T(8,128)S(1)} %get-tuple-element.29), channel_id=1, source_target_pairs={{4,0},{8,4},{12,8},{16,12},{20,16},{24,20},{28,24},{0,28},{5,1},{9... | collective-permute-start | bytes 884744 | tf_op jit(solution)/shard_map/ppermute | solution.py:27
  8.0 9.5 %collective-permute-done = f32[3,2,32,384]{3,2,1,0:T(8,128)S(1)} collective-permute-done((f32[3,2,32,384]{3,2,1,0:T(8,128)S(1)}, f32[3,2,32,384]{3,2,1,0:T(8,128)S(1)}, u32[]{:S(2)}, u32[]{:S(2)}) %collective-permute-start) | collective-permute-done | bytes 294944 | tf_op jit(solution)/shard_map/ppermute | solution.py:26
  17.5 0.1 constant_dynamic-update-slice_fusion.1
  17.6 2.1 %collective-permute-done.1 = f32[3,2,32,384]{3,2,1,0:T(8,128)S(1)} collective-permute-done((f32[3,2,32,384]{3,2,1,0:T(8,128)S(1)}, f32[3,2,32,384]{3,2,1,0:T(8,128)S(1)}, u32[]{:S(2)}, u32[]{:S(2)}) %collective-permute-start.1) | collective-permute-done | bytes 294944 | tf_op jit(solution)/shard_map/ppermute | solution.py:27
  19.8 0.5 collective-permute-start.2
  20.3 0.1 fusion.58
  20.4 1.8 %collective-permute-done.3 = f32[3,12,2,384]{3,2,1,0:T(2,128)S(1)} collective-permute-done((f32[3,12,2,384]{3,2,1,0:T(2,128)S(1)}, f32[3,12,2,384]{3,2,1,0:T(2,128)S(1)}, u32[]{:S(2)}, u32[]{:S(2)}) %collective-permute-start.3) | collective-permute-done | bytes 110624 | tf_op jit(solution)/shard_map/ppermute | solution.py:27
  22.3 3.0 %collective-permute-done.2 = f32[3,12,2,384]{3,2,1,0:T(2,128)S(1)} collective-permute-done((f32[3,12,2,384]{3,2,1,0:T(2,128)S(1)}, f32[3,12,2,384]{3,2,1,0:T(2,128)S(1)}, u32[]{:S(2)}, u32[]{:S(2)}) %collective-permute-start.2) | collective-permute-done | bytes 110624 | tf_op jit(solution)/shard_map/ppermute | solution.py:26
  25.2 0.3 pad_maximum_fusion
  25.5 0.3 fusion.15
  25.8 0.3 fusion.18
  26.0 0.5 fusion.16
  26.6 0.4 fusion.22
  27.1 1.3 %fusion.12 = (f32[3,10,34,384]{3,2,1,0:T(8,128)S(1)}, f32[3,10,34,384]{3,2,1,0:T(8,128)S(1)}) fusion(f32[3,10,34,384]{3,2,1,0:T(8,128)S(1)} %get-tuple-element.22, f32[384]{0:T(512)S(1)} %get-tuple-element.9, f32[3,12,32,384]{3,2,1,0:T(8,128)S(1)} %constant_dynamic-update-slice_fusion, f32[3,12,2,384]{3,2,1,0:T(2,128)S(1)} %collective-permute-done.2, ...), kind=kLoop, calls=%fused_computation.27 | loop fusion | flops 2350080 | bytes 6692352 | tf_op jit(solution)/shard_map/div | solution.py:34
  28.5 0.6 fusion.29
  29.2 0.1 multiply_dynamic-update-slice_fusion.1
  29.3 0.1 multiply_dynamic-update-slice_fusion
  29.4 0.3 broadcast_multiply_fusion
  29.6 0.4 fusion
  30.1 0.7 fusion.21
  30.8 0.4 fusion.36
  31.8 0.1 multiply_dynamic-update-slice_fusion.5
  31.9 0.1 multiply_dynamic-update-slice_fusion.4
  32.0 0.1 multiply_dynamic-update-slice_fusion.3
  32.2 0.4 fusion.2
  32.6 0.9 %fusion.9 = f32[6,8,32,384]{3,2,1,0:T(8,128)S(1)} fusion(f32[6,8,32,384]{3,2,1,0:T(8,128)S(1)} %multiply_dynamic-update-slice_fusion.12, f32[6,8,34,384]{3,2,1,0:T(8,128)S(1)} %fusion.2), kind=kLoop, calls=%fused_computation.21 | loop fusion | flops 3538944 | bytes 11796480 | tf_op jit(solution)/shard_map/sub | solution.py:79
  33.5 0.9 %fusion.6 = f32[6,8,32,384]{3,2,1,0:T(8,128)S(1)} fusion(f32[6,8,34,384]{3,2,1,0:T(8,128)S(1)} %fusion, f32[6,8,32,384]{3,2,1,0:T(8,128)S(1)} %multiply_dynamic-update-slice_fusion.9, f32[8,32,384]{2,1,0:T(8,128)S(1)} %get-tuple-element.19, f32[384]{0:T(512)S(1)} %get-tuple-element.8), kind=kLoop, calls=%fused_computation.15 | loop fusion | flops 4718592 | bytes 12191232 | tf_op jit(solution)/shard_map/mul | solution.py:80
  34.4 1.4 %fusion.65 = (f32[384]{0:T(512)S(1)}, f32[8,32,384]{2,1,0:T(8,128)}, f32[384]{0:T(512)S(1)}, f32[8,32,384]{2,1,0:T(8,128)}) fusion(f32[6,8,32,384]{3,2,1,0:T(8,128)S(1)} %fusion.6, f32[6,8,32,384]{3,2,1,0:T(8,128)S(1)} %fusion.9), kind=kLoop, calls=%fused_computation.156 | loop fusion | flops 2948352 | bytes 5508096 | tf_op jit(solution)/shard_map/reduce_sum | solution.py:112
  35.8 40.1 %all-gather.1 = f32[32,2,384]{2,1,0:T(2,128)S(1)} all-gather(f32[1,2,384]{2,1,0:T(2,128)S(1)} %maximum_bitcast_fusion), channel_id=2, replica_groups=mesh['gx'=8,'gz'=4] {'gx','gz'}, dimensions={0}, use_global_device_ids=true | all-gather | bytes 101376 | tf_op jit(solution)/shard_map/all_gather | solution.py:11
  76.0 1.1 %fusion.44 = f32[8,32,384]{2,1,0:T(8,128)} fusion(f32[10,34,384]{2,1,0:T(8,128)S(1)} %get-tuple-element.14, f32[10,34,384]{2,1,0:T(8,128)S(1)} %get-tuple-element.12, f32[10,34,384]{2,1,0:T(8,128)S(1)} %get-tuple-element.16, f32[10,34,384]{2,1,0:T(8,128)S(1)} %broadcast_multiply_fusion.1, f32[10,34,384]{2,1,0:T(8,128)S(1)} %bitcast.71, f32[384]{0:T(512)S(1)} %fusion.57), kind=kLoop, calls=%fused_computation.103 | loop fusion | flops 983040 | bytes 2360832 | tf_op jit(solution)/shard_map/mul | solution.py:115
  (34 shorter events, 1.2 us)
Async XLA Ops:
  0.6 16.8 %copy-start = (f32[3,8,32,384]{3,2,1,0:T(8,128)S(1)}, f32[3,8,32,384]{3,2,1,0:T(8,128)}, u32[]{:S(2)}) copy-start(f32[3,8,32,384]{3,2,1,0:T(8,128)} %param.2) | copy-start | bytes 3538948
  0.6 19.7 %copy-start.2 = (f32[385]{0:T(512)S(1)}, f32[385]{0:T(512)}, u32[]{:S(2)}) copy-start(f32[385]{0:T(512)} %param.3) | copy-start | bytes 4624
  1.8 15.6 %collective-permute-start = (f32[3,2,32,384]{3,2,1,0:T(8,128)S(1)}, f32[3,2,32,384]{3,2,1,0:T(8,128)S(1)}, u32[]{:S(2)}, u32[]{:S(2)}) collective-permute-start(f32[3,2,32,384]{3,2,1,0:T(8,128)S(1)} %get-tuple-element.30), channel_id=1, source_target_pairs={{0,4},{4,8},{8,12},{12,16},{16,20},{20,24},{24,28},{28,0},{1,5},{5... | collective-permute-start | bytes 884744 | tf_op jit(solution)/shard_map/ppermute | solution.py:26
  4.9 14.8 %collective-permute-start.1 = (f32[3,2,32,384]{3,2,1,0:T(8,128)S(1)}, f32[3,2,32,384]{3,2,1,0:T(8,128)S(1)}, u32[]{:S(2)}, u32[]{:S(2)}) collective-permute-start(f32[3,2,32,384]{3,2,1,0:T(8,128)S(1)} %get-tuple-element.29), channel_id=1, source_target_pairs={{4,0},{8,4},{12,8},{16,12},{20,16},{24,20},{28,24},{0,28},{5,1},{9... | collective-permute-start | bytes 884744 | tf_op jit(solution)/shard_map/ppermute | solution.py:27
  19.8 2.5 %collective-permute-start.3 = (f32[3,12,2,384]{3,2,1,0:T(2,128)S(1)}, f32[3,12,2,384]{3,2,1,0:T(2,128)S(1)}, u32[]{:S(2)}, u32[]{:S(2)}) collective-permute-start(f32[3,12,2,384]{3,2,1,0:T(2,128)S(1)} %get-tuple-element.28), channel_id=1, source_target_pairs={{1,0},{2,1},{3,2},{0,3},{5,4},{6,5},{7,6},{4,7},{9,8},{10,9},{11,1... | collective-permute-start | bytes 331784 | tf_op jit(solution)/shard_map/ppermute | solution.py:27
  19.8 5.4 %collective-permute-start.2 = (f32[3,12,2,384]{3,2,1,0:T(2,128)S(1)}, f32[3,12,2,384]{3,2,1,0:T(2,128)S(1)}, u32[]{:S(2)}, u32[]{:S(2)}) collective-permute-start(f32[3,12,2,384]{3,2,1,0:T(2,128)S(1)} %get-tuple-element.27), channel_id=1, source_target_pairs={{0,1},{1,2},{2,3},{3,0},{4,5},{5,6},{6,7},{7,4},{8,9},{9,10},{10,1... | collective-permute-start | bytes 331784 | tf_op jit(solution)/shard_map/ppermute | solution.py:26
  76.0 1.2 %copy-start.1 = (f32[384]{0:T(512)}, f32[384]{0:T(512)S(1)}, u32[]{:S(2)}) copy-start(f32[384]{0:T(512)S(1)} %fusion.61) | copy-start | bytes 4612
